TPU v7x, 128 devices: a whole 4x4x4 slice. The times are simulated.
128 devices in a mesh: row: 16 (over y_lo, x, core), col: 8 (over y_hi, z).
Axes of the slice: x: 4, y: 4 (y_hi: 2, y_lo: 2; y = y_hi * 2 + y_lo), z: 4, core: 2. Of those that a mesh axis runs over, the one named last changes fastest.
Arguments:
- tokens: bfloat16 [2048, 8192], P('row', 'col'), may hold values from -6 to 6
- weights: bfloat16 [2, 14336, 8192], P(None, 'row', 'col'), may hold values from -0.0625 to 0.0625
- gradients: bfloat16 [2, 14336, 8192], P(None, 'row', 'col'), may hold values from -200 to 200, as said below
- row_factors: float32 [2, 14336], P(None, 'row'), may hold values from 0.05 to 0.5
- col_factors: float32 [2, 8192], P(None, 'col'), may hold values from 0.05 to 0.5
Outputs:
- hidden: bfloat16 [2048, 14336], P('col', 'row')
- row_new: float32 [2, 14336], P(None, 'row')
- col_new: float32 [2, 8192], P(None, 'col')
Inputs may be any that keep to these rules, and one draw needn't show every extreme that they name: Finite real gradients.
All inputs are finite; a program needn't handle non-finite values.
Results may differ from a plain program's by a relative error of at most 0.001.
The roundings to bfloat16 on the way count: a program that leaves them out, or rounds other values in their place, can miss the bound.
Values may be sent and summed in bfloat16 or wider, within the bound.
A program may use at most 128 MiB of HBM per device.

v0:
```python
import jax
import jax.numpy as jnp
from jax import lax
from jax.sharding import Mesh
from jax.sharding import PartitionSpec as P

D = 8192
FF = 14336
COL = ("col_0", "col_1")
ROW = ("row_0", "row_1", "row_2")
ROW_COL = ("row_0", "row_1", "row_2", "col_0", "col_1")
decay_rate = 0.5
learn_rate = 0.01
clip_limit = 1.0
tiny_eps = 1e-30


def copy_for_each(x, axis):
    copies = jnp.broadcast_to(x, (lax.axis_size(axis), *x.shape))
    return lax.all_to_all(copies, axis, split_axis=0, concat_axis=0, tiled=True)


def taken_together(x, axis):
    everything = copy_for_each(x, axis)
    return jnp.sum(everything, axis=0)


def by_axis(x, axes):
    for axis in axes:
        x = lax.psum(x, axis)
    return x


def local(tokens, weights, gradients, row_factors, col_factors):
    gradient = gradients.astype(jnp.float32)
    squares = gradient * gradient
    row_part = jnp.sum(squares, axis=2)
    col_part = jnp.sum(squares, axis=1)
    row_block = row_part.shape[1]
    col_block = col_part.shape[1]
    row_total = taken_together(row_part, COL)
    col_total = taken_together(col_part, ROW)
    row_new = decay_rate * row_factors + (1.0 - decay_rate) * (row_total / D + tiny_eps)
    col_new = decay_rate * col_factors + (1.0 - decay_rate) * (col_total / FF + tiny_eps)
    row_mean = taken_together(jnp.sum(row_new, axis=1), ROW) / FF
    denominator = jnp.sqrt(row_new[:, :, None] * col_new[:, None, :] / row_mean[:, None, None])
    update = gradient / denominator
    norm_total = by_axis(jnp.sum(update * update, axis=(1, 2)), ROW_COL)
    clip_scale = jnp.maximum(1.0, jnp.sqrt(norm_total / (FF * D)) / clip_limit)
    new_weights = (
        weights.astype(jnp.float32) - learn_rate * update / clip_scale[:, None, None]
    ).astype(jnp.bfloat16)
    spread = lax.all_gather(tokens, ROW, axis=0, tiled=True)
    flat_weights = new_weights.reshape(2 * row_block, col_block)
    combined = lax.psum_scatter(
        lax.dot_general(
            spread, flat_weights, (((1,), (1,)), ((), ())), preferred_element_type=jnp.float32
        ),
        COL,
        scatter_dimension=0,
        tiled=True,
    )
    gate_proj = combined[:, :row_block]
    up_proj = combined[:, row_block:]
    hidden = (jax.nn.silu(gate_proj) * up_proj).astype(jnp.bfloat16)
    return (hidden, row_new, col_new)


def solution(mesh):
    torus = Mesh(mesh.devices.reshape(2, 4, 2, 2, 4), ("row_0", "row_1", "row_2", "col_0", "col_1"))
    in_specs = (P(ROW, COL), P(None, ROW, COL), P(None, ROW, COL), P(None, ROW), P(None, COL))
    out_specs = (P(COL, ROW), P(None, ROW), P(None, COL))
    return jax.shard_map(local, mesh=torus, in_specs=in_specs, out_specs=out_specs, check_vma=False)
```

profile of v0, /device:TPU:0, one launch (start us, length us, event | category | flops | bytes accessed | tf_op | source)
XLA Modules:
  0.0 280.4 jit_solution(5089476382716384147)
XLA Ops:
  7.2 0.0 all-gather.2.cloned.1.call-start
  7.2 0.7 all-gather.2.cloned.1.call-update
  7.9 3.1 %fusion = (f32[2,1024]{1,0:T(2,128)S(1)}, f32[2,896]{1,0:T(2,128)S(1)}) fusion(bf16[2,896,1024]{2,1,0:T(8,128)(2,1)} %param.7), kind=kLoop, calls=%fused_computation.2 | loop fusion | flops 7336192 | bytes 3685376 | tf_op jit(solution)/shard_map/reduce_sum | solution.py:38
  11.0 15.7 %all_to_all.16 = f32[8,2,896]{2,1,0:T(2,128)S(1)} all-to-all(f32[8,2,896]{2,1,0:T(2,128)S(1)} %broadcast_in_dim.6), channel_id=1, replica_groups=mesh['row_0'=2,'row_1'=4,'row_2'=2,'col_0'=2,'col_1'=4] {'col_0','col_1'}, dimensions={0} | all-to-all | bytes 114688 | tf_op jit(solution)/shard_map/all_to_all | solution.py:20
  26.7 0.8 fusion.3
  27.5 0.0 copy-start.1
  27.6 10.4 %all_to_all.17 = f32[16,1,2]{2,1,0:T(1,128)S(1)} all-to-all(f32[16,1,2]{2,1,0:T(1,128)S(1)} %broadcast_in_dim.15), channel_id=1, replica_groups=mesh['row_0'=2,'row_1'=4,'row_2'=2,'col_0'=2,'col_1'=4] {'row_0','row_1'..., dimensions={0} | all-to-all | bytes 256 | tf_op jit(solution)/shard_map/all_to_all | solution.py:20
  38.0 0.7 broadcast_in_dim.14
  38.7 3.5 %all-to-all-start.1 = ((f32[16,2,1024]{2,1,0:T(2,128)}), f32[16,2,1024]{2,1,0:T(2,128)S(1)}, u32[]{:S(2)}, u32[]{:S(2)}) async-start(f32[16,2,1024]{2,1,0:T(2,128)} %broadcast_in_dim.14), calls=%async_computation.1 | async-start | bytes 262144 | tf_op jit(solution)/shard_map/all_to_all | solution.py:20
  42.2 0.0 reduce-scatter.2.cloned.1.call-start
  42.3 6.2 %all-to-all-done.1 = f32[16,2,1024]{2,1,0:T(2,128)S(1)} async-done(((f32[16,2,1024]{2,1,0:T(2,128)}), f32[16,2,1024]{2,1,0:T(2,128)S(1)}, u32[]{:S(2)}, u32[]{:S(2)}) %all-to-all-start.1) | async-done | bytes 131104 | tf_op jit(solution)/shard_map/all_to_all | solution.py:20
  48.5 0.1 reduce_sum.66
  48.6 0.7 add_multiply_fusion
  49.3 0.0 copy-start
  49.3 4.6 %multiply_reduce_fusion = f32[2]{0:T(128)S(1)} fusion(f32[2]{0:T(128)S(1)} %broadcast_multiply_fusion, f32[2,1024]{1,0:T(2,128)S(1)} %add_multiply_fusion, f32[2,896]{1,0:T(2,128)S(1)} %get-tuple-element.15, bf16[2,896,1024]{2,1,0:T(8,128)(2,1)} %param.7), kind=kLoop, calls=%fused_computation.6 | loop fusion | flops 11010046 | bytes 3685392 | tf_op jit(solution)/shard_map/reduce_sum | solution.py:48
  53.9 4.9 %psum.35 = f32[2]{0:T(128)S(1)} all-reduce(f32[2]{0:T(128)S(1)} %multiply_reduce_fusion), channel_id=1, replica_groups=mesh['row_0'=2,'row_1'=4,'row_2'=2,'col_0'=2,'col_1'=4] {'row_0'}, use_global_device_ids=true, to_apply=%region_7.0 | all-reduce | flops 2 | bytes 16 | tf_op jit(solution)/shard_map/psum | solution.py:30
  58.8 9.5 %psum.36 = f32[2]{0:T(128)S(1)} all-reduce(f32[2]{0:T(128)S(1)} %psum.35), channel_id=1, replica_groups=mesh['row_0'=2,'row_1'=4,'row_2'=2,'col_0'=2,'col_1'=4] {'row_1'}, use_global_device_ids=true, to_apply=%region_8.0 | all-reduce | flops 2 | bytes 16 | tf_op jit(solution)/shard_map/psum | solution.py:30
  68.3 2.5 psum.37
  70.8 6.4 %psum.38 = f32[2]{0:T(128)S(1)} all-reduce(f32[2]{0:T(128)S(1)} %psum.37), channel_id=1, replica_groups=mesh['row_0'=2,'row_1'=4,'row_2'=2,'col_0'=2,'col_1'=4] {'col_0'}, use_global_device_ids=true, to_apply=%region_10.0 | all-reduce | flops 2 | bytes 16 | tf_op jit(solution)/shard_map/psum | solution.py:30
  77.2 8.6 %psum.39 = f32[2]{0:T(128)S(1)} all-reduce(f32[2]{0:T(128)S(1)} %psum.38), channel_id=1, replica_groups=mesh['row_0'=2,'row_1'=4,'row_2'=2,'col_0'=2,'col_1'=4] {'col_1'}, use_global_device_ids=true, to_apply=%region_11.0 | all-reduce | flops 2 | bytes 16 | tf_op jit(solution)/shard_map/psum | solution.py:30
  85.8 5.7 %subtract_convert_fusion = bf16[2,896,1024]{2,1,0:T(8,128)(2,1)} fusion(bf16[2,896,1024]{2,1,0:T(8,128)(2,1)} %param.6, f32[2]{0:T(128)S(1)} %sqrt_maximum_fusion, f32[2]{0:T(128)S(1)} %broadcast_multiply_fusion, f32[2,1024]{1,0:T(2,128)S(1)} %add_multiply_fusion, f32[2,896]{1,0:T(2,128)S(1)} %get-tuple-element.15, bf16[2,896,1024]{2,1,0:T(8,128)(2,1)} %param.7), kind=kLoop, calls=%fused_computation.5 | loop fusion | flops 16515072 | bytes 11025424 | tf_op jit(solution)/shard_map/convert_element_type | solution.py:52
  91.5 0.0 copy-done.1
  91.5 0.0 copy-done
  91.5 0.0 all-gather.2.cloned.1.call-done
  91.6 13.8 %convolution_bitcast_fusion = f32[2048,1792]{0,1:T(8,128)} fusion(bf16[1792,1024]{1,0:T(8,128)(2,1)} %bitcast.5, bf16[2048,1024]{1,0:T(8,128)(2,1)} %all-gather.2.cloned.1.call-done), kind=kOutput, calls=%fused_computation.4 | convolution fusion | flops 7516192768 | bytes 22544384 | tf_op jit(solution)/shard_map/dot_general | solution.py:56
  105.4 0.0 reduce-scatter.2.cloned.1.call-update
  105.4 165.5 %reduce-scatter.2.cloned.1.call-done = f32[256,1792]{0,1:T(8,128)} async-done(((f32[2048,1792]{0,1:T(8,128)}), f32[256,1792]{0,1:T(8,128)}) %reduce-scatter.2.cloned.1.call-update) | async-done | bytes 1835024 | tf_op jit(solution)/shard_map/reduce_scatter | solution.py:55
  270.9 1.7 fusion.2
  272.6 1.0 copy.13
  (6 shorter events, 0.1 us)
Async XLA Ops:
  7.2 84.4 %all-gather.2.cloned.1.call-start = ((), (), s32[]{:S(2)}) async-start(), calls=%async_computation.4 | async-start | bytes 4456448 | tf_op jit(solution)/shard_map/all_gather | solution.py:53
  27.5 64.0 %copy-start.1 = (f32[2,896]{1,0:T(2,128)}, f32[2,896]{1,0:T(2,128)S(1)}, u32[]{:S(2)}) copy-start(f32[2,896]{1,0:T(2,128)S(1)} %get-tuple-element.15) | copy-start | bytes 21508
  38.7 9.9 %all-to-all-start.1 = ((f32[16,2,1024]{2,1,0:T(2,128)}), f32[16,2,1024]{2,1,0:T(2,128)S(1)}, u32[]{:S(2)}, u32[]{:S(2)}) async-start(f32[16,2,1024]{2,1,0:T(2,128)} %broadcast_in_dim.14), calls=%async_computation.1 | async-start | bytes 262144 | tf_op jit(solution)/shard_map/all_to_all | solution.py:20
  42.2 228.7 %reduce-scatter.2.cloned.1.call-start = ((), (), s32[]{:S(2)}) async-start(), calls=%async_computation.5 | async-start | bytes 16515072 | tf_op jit(solution)/shard_map/reduce_scatter | solution.py:55
  49.3 42.3 %copy-start = (f32[2,1024]{1,0:T(2,128)}, f32[2,1024]{1,0:T(2,128)S(1)}, u32[]{:S(2)}) copy-start(f32[2,1024]{1,0:T(2,128)S(1)} %add_multiply_fusion) | copy-start | bytes 24580
Sparse Core Ops, SparseCore 0:
  9.7 39.8 all-gather.1
  105.5 165.3 reduce-scatter.1
where the time goes:
time: 281 us; the launch traced here: 280 us
  waiting for transfers between devices  172 us (61%)
  blocking collectives  58 us (21%)
  other arithmetic  16.8 us (6%)
  between operations  14.1 us (5%)
  matrix products  13.8 us (5%)
  starting transfers between devices  3.59 us (1%)
    reduce_scatter x1, waiting for transfers between devices, local(): lax.psum_scatter(lax.dot_general(spread, flat_weights, (((1,), (1,)), (()...  166 us
    psum x5, blocking collectives, by_axis(): x = lax.psum(x, axis)  31.9 us
    all_to_all x2, blocking collectives, copy_for_each(): return lax.all_to_all(copies, axis, split_axis=0, concat_axis=0, tiled=True)  26.1 us
    dot_general x1, matrix products, local(): lax.dot_general(spread, flat_weights, (((1,), (1,)), ((), ())), preferred...  13.8 us
    all_to_all x1, waiting for transfers between devices, copy_for_each(): return lax.all_to_all(copies, axis, split_axis=0, concat_axis=0, tiled=True)  6.24 us
    convert_element_type x1, other arithmetic, local(): new_weights = (weights.astype(jnp.float32) - learn_rate * update / clip_s...  5.73 us
  transfers between devices with their start and end apart: 3, of which 2 were waited for; matrix products, arithmetic and copies ran while one was open for 6% of the time, Pallas kernels for 0%

commit v1 on v0

--- a/solution.py
+++ b/solution.py
@@ -27,7 +27,7 @@
 
 def by_axis(x, axes):
     for axis in axes:
-        x = lax.psum(x, axis)
+        x = jnp.sum(lax.all_gather(x, axis), axis=0)
     return x
 
 

time: 281 us -> 289 us (1.028)
  blocking collectives: 58 us -> 32.6 us
  starting transfers between devices: 3.59 us -> 16 us
  local copies, waits for them, and re-layouts: 1.7 us -> 10.9 us
  waiting for transfers between devices: 172 us -> 181 us
  between operations: 14.1 us -> 17.3 us
    unnamed x0 -> x5, blocking collectives: none -> 32.6 us
    psum x5 -> x0, blocking collectives: 31.9 us -> none  [by_axis(): x = lax.psum(x, axis)]
    all_to_all x2 -> x0, blocking collectives: 26.1 us -> none  [copy_for_each(): return lax.all_to_all(copies, axis, split_axis=0, concat_axis=0, tiled=True)]
    all_to_all x1 -> x3, starting transfers between devices: 3.51 us -> 16 us  [copy_for_each(): return lax.all_to_all(copies, axis, split_axis=0, concat_axis=0, tiled=True)]
    unnamed x5 -> x20, local copies, waits for them, and re-layouts: 0.99 us -> 8.52 us
    all_to_all x1 -> x3, waiting for transfers between devices: 6.24 us -> 13.2 us  [copy_for_each(): return lax.all_to_all(copies, axis, split_axis=0, concat_axis=0, tiled=True)]
  transfers between devices with their start and end apart: 3 -> 5, of which waited for: 2 -> 4; matrix products, arithmetic and copies ran while one was open for 6% -> 9% of each run, Pallas kernels for 0% -> 0%
where the time goes in v1:
time: 289 us; the launch traced here: 288 us
  waiting for transfers between devices  181 us (63%)
  blocking collectives  32.6 us (11%)
  between operations  17.3 us (6%)
  other arithmetic  16.9 us (6%)
  starting transfers between devices  16 us (6%)
  matrix products  13.8 us (5%)
  local copies, waits for them, and re-layouts  10.9 us (4%)
    reduce_scatter x1, waiting for transfers between devices, local(): lax.psum_scatter(lax.dot_general(spread, flat_weights, (((1,), (1,)), (()...  167 us
    unnamed x5, blocking collectives  32.6 us
    all_to_all x3, starting transfers between devices, copy_for_each(): return lax.all_to_all(copies, axis, split_axis=0, concat_axis=0, tiled=True)  16 us
    dot_general x1, matrix products, local(): lax.dot_general(spread, flat_weights, (((1,), (1,)), ((), ())), preferred...  13.8 us
    all_to_all x3, waiting for transfers between devices, copy_for_each(): return lax.all_to_all(copies, axis, split_axis=0, concat_axis=0, tiled=True)  13.2 us
    unnamed x20, local copies, waits for them, and re-layouts  8.52 us
  transfers between devices with their start and end apart: 5, of which 4 were waited for; matrix products, arithmetic and copies ran while one was open for 9% of the time, Pallas kernels for 0%

profile of v1, /device:TPU:0, one launch (start us, length us, event | category | flops | bytes accessed | tf_op | source)
XLA Modules:
  0.0 288.4 jit_solution(4667887581129877913)
XLA Ops:
  7.2 0.0 all-gather.7.cloned.1.call-start
  7.2 0.7 all-gather.7.cloned.1.call-update
  7.9 3.1 %fusion = (f32[2,1024]{1,0:T(2,128)S(1)}, f32[2,896]{1,0:T(2,128)S(1)}) fusion(bf16[2,896,1024]{2,1,0:T(8,128)(2,1)} %param.7), kind=kLoop, calls=%fused_computation.2 | loop fusion | flops 7336192 | bytes 3685376 | tf_op jit(solution)/shard_map/reduce_sum | solution.py:38
  11.0 0.6 broadcast_in_dim.6
  11.6 8.1 %all-to-all-start = ((f32[8,2,896]{2,1,0:T(2,128)}), f32[8,2,896]{2,1,0:T(2,128)S(1)}, u32[]{:S(2)}, u32[]{:S(2)}) async-start(f32[8,2,896]{2,1,0:T(2,128)} %broadcast_in_dim.6), calls=%async_computation | async-start | bytes 114688 | tf_op jit(solution)/shard_map/all_to_all | solution.py:20
  19.7 1.3 dynamic-slice.4
  21.0 1.2 dynamic-slice.3
  22.2 1.3 dynamic-slice.2
  23.5 1.3 dynamic-slice.1
  24.8 1.3 dynamic-slice
  26.1 1.6 all-to-all-done
  27.7 0.8 fusion.3
  28.5 0.0 copy-start.1
  28.5 0.6 broadcast_in_dim.15
  29.1 4.4 %all-to-all-start.2 = ((f32[16,1,2]{2,1,0:T(1,128)}), f32[16,1,2]{2,1,0:T(1,128)S(1)}, u32[]{:S(2)}, u32[]{:S(2)}) async-start(f32[16,1,2]{2,1,0:T(1,128)} %broadcast_in_dim.15), calls=%async_computation.2 | async-start | bytes 16384 | tf_op jit(solution)/shard_map/all_to_all | solution.py:20
  34.1 5.4 %all-to-all-done.2 = f32[16,1,2]{2,1,0:T(1,128)S(1)} async-done(((f32[16,1,2]{2,1,0:T(1,128)}), f32[16,1,2]{2,1,0:T(1,128)S(1)}, u32[]{:S(2)}, u32[]{:S(2)}) %all-to-all-start.2) | async-done | bytes 160 | tf_op jit(solution)/shard_map/all_to_all | solution.py:20
  39.5 0.7 broadcast_in_dim.14
  40.2 3.5 %all-to-all-start.1 = ((f32[16,2,1024]{2,1,0:T(2,128)}), f32[16,2,1024]{2,1,0:T(2,128)S(1)}, u32[]{:S(2)}, u32[]{:S(2)}) async-start(f32[16,2,1024]{2,1,0:T(2,128)} %broadcast_in_dim.14), calls=%async_computation.1 | async-start | bytes 262144 | tf_op jit(solution)/shard_map/all_to_all | solution.py:20
  43.7 0.0 reduce-scatter.2.cloned.1.call-start
  43.8 6.2 %all-to-all-done.1 = f32[16,2,1024]{2,1,0:T(2,128)S(1)} async-done(((f32[16,2,1024]{2,1,0:T(2,128)}), f32[16,2,1024]{2,1,0:T(2,128)S(1)}, u32[]{:S(2)}, u32[]{:S(2)}) %all-to-all-start.1) | async-done | bytes 131104 | tf_op jit(solution)/shard_map/all_to_all | solution.py:20
  50.1 0.1 reduce_sum.111
  50.1 0.7 add_multiply_fusion
  50.8 0.0 copy-start
  50.8 4.6 %multiply_reduce_fusion = f32[2]{0:T(128)S(1)} fusion(f32[2]{0:T(128)S(1)} %broadcast_multiply_fusion, f32[2,1024]{1,0:T(2,128)S(1)} %add_multiply_fusion, f32[2,896]{1,0:T(2,128)S(1)} %get-tuple-element.18, bf16[2,896,1024]{2,1,0:T(8,128)(2,1)} %param.7), kind=kLoop, calls=%fused_computation.6 | loop fusion | flops 11010046 | bytes 3685392 | tf_op jit(solution)/shard_map/reduce_sum | solution.py:48
  55.5 0.2 dynamic-update-slice
  56.3 4.9 %all-reduce = f32[4]{0:T(128)S(1)} all-reduce(f32[4]{0:T(128)S(1)} %dynamic-update-slice), channel_id=2, replica_groups=mesh['row_0'=2,'row_1'=4,'row_2'=2,'col_0'=2,'col_1'=4] {'row_0'}, use_global_device_ids=true, to_apply=%add | all-reduce | flops 4 | bytes 32
  61.2 0.1 reshape.24
  61.3 0.2 dynamic-update-slice.1
  62.2 9.2 %all-reduce.1 = f32[8]{0:T(128)S(1)} all-reduce(f32[8]{0:T(128)S(1)} %dynamic-update-slice.1), channel_id=3, replica_groups=mesh['row_0'=2,'row_1'=4,'row_2'=2,'col_0'=2,'col_1'=4] {'row_1'}, use_global_device_ids=true, to_apply=%add.1 | all-reduce | flops 8 | bytes 64
  71.4 0.1 reshape.25
  71.5 0.2 dynamic-update-slice.2
  72.3 2.5 all-reduce.2
  74.8 0.1 reshape.26
  74.9 0.2 dynamic-update-slice.3
  75.8 6.4 %all-reduce.3 = f32[4]{0:T(128)S(1)} all-reduce(f32[4]{0:T(128)S(1)} %dynamic-update-slice.3), channel_id=5, replica_groups=mesh['row_0'=2,'row_1'=4,'row_2'=2,'col_0'=2,'col_1'=4] {'col_0'}, use_global_device_ids=true, to_apply=%add.3 | all-reduce | flops 4 | bytes 32
  82.3 0.1 reshape.27
  82.4 0.2 dynamic-update-slice.4
  82.6 9.5 %all-reduce.4 = f32[8]{0:T(128)S(1)} all-reduce(f32[8]{0:T(128)S(1)} %dynamic-update-slice.4), channel_id=6, replica_groups=mesh['row_0'=2,'row_1'=4,'row_2'=2,'col_0'=2,'col_1'=4] {'col_1'}, use_global_device_ids=true, to_apply=%add.4 | all-reduce | flops 8 | bytes 64
  92.2 0.1 reshape.28
  92.3 5.7 %subtract_convert_fusion = bf16[2,896,1024]{2,1,0:T(8,128)(2,1)} fusion(bf16[2,896,1024]{2,1,0:T(8,128)(2,1)} %param.6, f32[2]{0:T(128)S(1)} %sqrt_maximum_fusion, f32[2]{0:T(128)S(1)} %broadcast_multiply_fusion, f32[2,1024]{1,0:T(2,128)S(1)} %add_multiply_fusion, f32[2,896]{1,0:T(2,128)S(1)} %get-tuple-element.18, bf16[2,896,1024]{2,1,0:T(8,128)(2,1)} %param.7), kind=kLoop, calls=%fused_computation.5 | loop fusion | flops 16515072 | bytes 11025424 | tf_op jit(solution)/shard_map/convert_element_type | solution.py:52
  98.0 0.0 copy-done.1
  98.0 0.0 copy-done
  98.0 0.0 all-gather.7.cloned.1.call-done
  98.0 13.8 %convolution_bitcast_fusion = f32[2048,1792]{0,1:T(8,128)} fusion(bf16[1792,1024]{1,0:T(8,128)(2,1)} %bitcast.10, bf16[2048,1024]{1,0:T(8,128)(2,1)} %all-gather.7.cloned.1.call-done), kind=kOutput, calls=%fused_computation.4 | convolution fusion | flops 7516192768 | bytes 22544384 | tf_op jit(solution)/shard_map/dot_general | solution.py:56
  111.8 0.0 reduce-scatter.2.cloned.1.call-update
  111.9 167.0 %reduce-scatter.2.cloned.1.call-done = f32[256,1792]{0,1:T(8,128)} async-done(((f32[2048,1792]{0,1:T(8,128)}), f32[256,1792]{0,1:T(8,128)}) %reduce-scatter.2.cloned.1.call-update) | async-done | bytes 1835024 | tf_op jit(solution)/shard_map/reduce_scatter | solution.py:55
  278.8 1.7 fusion.2
  280.5 1.0 copy.14
  (14 shorter events, 0.2 us)
Async XLA Ops:
  7.2 90.9 %all-gather.7.cloned.1.call-start = ((), (), s32[]{:S(2)}) async-start(), calls=%async_computation.4 | async-start | bytes 4456448 | tf_op jit(solution)/shard_map/all_gather | solution.py:53
  11.6 16.0 %all-to-all-start = ((f32[8,2,896]{2,1,0:T(2,128)}), f32[8,2,896]{2,1,0:T(2,128)S(1)}, u32[]{:S(2)}, u32[]{:S(2)}) async-start(f32[8,2,896]{2,1,0:T(2,128)} %broadcast_in_dim.6), calls=%async_computation | async-start | bytes 114688 | tf_op jit(solution)/shard_map/all_to_all | solution.py:20
  28.5 69.5 %copy-start.1 = (f32[2,896]{1,0:T(2,128)}, f32[2,896]{1,0:T(2,128)S(1)}, u32[]{:S(2)}) copy-start(f32[2,896]{1,0:T(2,128)S(1)} %get-tuple-element.18) | copy-start | bytes 21508
  29.1 10.4 %all-to-all-start.2 = ((f32[16,1,2]{2,1,0:T(1,128)}), f32[16,1,2]{2,1,0:T(1,128)S(1)}, u32[]{:S(2)}, u32[]{:S(2)}) async-start(f32[16,1,2]{2,1,0:T(1,128)} %broadcast_in_dim.15), calls=%async_computation.2 | async-start | bytes 16384 | tf_op jit(solution)/shard_map/all_to_all | solution.py:20
  40.2 9.8 %all-to-all-start.1 = ((f32[16,2,1024]{2,1,0:T(2,128)}), f32[16,2,1024]{2,1,0:T(2,128)S(1)}, u32[]{:S(2)}, u32[]{:S(2)}) async-start(f32[16,2,1024]{2,1,0:T(2,128)} %broadcast_in_dim.14), calls=%async_computation.1 | async-start | bytes 262144 | tf_op jit(solution)/shard_map/all_to_all | solution.py:20
  43.7 235.1 %reduce-scatter.2.cloned.1.call-start = ((), (), s32[]{:S(2)}) async-start(), calls=%async_computation.5 | async-start | bytes 16515072 | tf_op jit(solution)/shard_map/reduce_scatter | solution.py:55
  50.8 47.2 %copy-start = (f32[2,1024]{1,0:T(2,128)}, f32[2,1024]{1,0:T(2,128)S(1)}, u32[]{:S(2)}) copy-start(f32[2,1024]{1,0:T(2,128)S(1)} %add_multiply_fusion) | copy-start | bytes 24580
Sparse Core Ops, SparseCore 0:
  9.7 40.5 all-gather.6
  112.0 166.7 reduce-scatter.1
